TPU v7x, 128 devices: a whole 4x4x4 slice. The times are simulated.
128 devices in a mesh: depth: 2 (over core), row: 16 (over z, x), col: 4 (over y).
Axes of the slice: x: 4, y: 4, z: 4, core: 2. Of those that a mesh axis runs over, the one named last changes fastest.
Arguments:
- right_side: bfloat16 [4, 16, 8, 128, 512], P(None, 'row', ('depth', 'col')), may hold values from -6 to 6
- inverse_diag: bfloat16 [4, 16, 8, 1, 128, 128], P(None, 'row', ('depth', 'col')), may hold values from -2 to 2.5, as said below
- coupling: bfloat16 [3, 16, 1024, 8, 2048], P(None, 'row', None, ('depth', 'col')), may hold values from -0.0625 to 0.0625
- pattern: int32 [3, 16, 8, 8, 16], P(None, 'row', None, ('depth', 'col')), may hold values 0 or 1
Outputs:
- forward_solution: bfloat16 [4, 16, 8, 128, 512], P(None, 'row', ('depth', 'col'))
- solution: bfloat16 [4, 16, 8, 128, 512], P(None, 'row', ('depth', 'col'))
Inputs may be any that keep to these rules, and one draw needn't show every extreme that they name: `inverse_diag`: each block is lower triangular with positive diagonal.
All inputs are finite; a program needn't handle non-finite values. No bound on the sum of `pattern` on one device may be relied on, other than what follows from the above.
Results may differ from a plain program's by a relative error of at most 0.025.
Values may be sent and summed in bfloat16 or wider, within the bound.
A program may use at most 128 MiB of HBM per device.

v0:
```python
import jax
import jax.numpy as jnp
from jax import lax
from jax.sharding import PartitionSpec as P


def apply_inverse(inverse, vector, transposed):
    blocks_in = vector.reshape(inverse.shape[0], inverse.shape[1], vector.shape[-1])
    einsum_form = "tji,tjn->tin" if transposed else "tij,tjn->tin"
    result = jnp.einsum(einsum_form, inverse, blocks_in, preferred_element_type=jnp.float32)
    return result.astype(jnp.bfloat16).reshape(vector.shape)


def lift_upward(masked, share_in):
    portion = lax.all_gather(share_in, "row", axis=0, tiled=True)
    span_rows = portion.shape[0] * portion.shape[2]
    return jnp.dot(
        masked, portion.reshape(span_rows, portion.shape[-1]), preferred_element_type=jnp.float32
    )


def carry_downward(masked, share_in):
    portion = lax.all_gather(share_in, ("depth", "col"), axis=1, tiled=True)
    span_rows = portion.shape[1] * portion.shape[2]
    return lax.dot_general(
        masked,
        portion.reshape(span_rows, portion.shape[-1]),
        (((0,), (0,)), ((), ())),
        preferred_element_type=jnp.float32,
    )


def forward_sum(partial_value, share_rows):
    blocks = partial_value.reshape(
        lax.axis_size(("depth", "col")), share_rows, partial_value.shape[-1]
    )
    summed = lax.psum(blocks.astype(jnp.bfloat16), ("depth", "col")).astype(jnp.float32)
    return lax.dynamic_index_in_dim(summed, lax.axis_index(("depth", "col")), 0, keepdims=False)


def backward_sum(partial_value, share_rows):
    blocks = partial_value.reshape(lax.axis_size("row"), share_rows, partial_value.shape[-1])
    summed = lax.psum(blocks.astype(jnp.bfloat16), "row").astype(jnp.float32)
    return lax.dynamic_index_in_dim(summed, lax.axis_index("row"), 0, keepdims=False)


def body(right_side, inverse_diag, coupling, pattern):
    levels = right_side.shape[0]
    share_rows = right_side.shape[3]
    rhs_cols = right_side.shape[4]
    block_width = inverse_diag.shape[-1]
    masked = []
    for pair_at in range(levels - 1):
        slab = coupling[pair_at, 0, :, 0, :]
        gate = pattern[pair_at, 0, :, 0, :].astype(jnp.bfloat16)
        shaped = (
            slab.reshape(gate.shape[0], block_width, gate.shape[1], block_width)
            * gate[:, None, :, None]
        )
        masked.append(shaped.reshape(slab.shape))
    panel_spans = [(0, rhs_cols)]
    fwd_levels = []
    for level_at in range(levels):
        pieces = []
        for panel_at, (col_first, col_last) in enumerate(panel_spans):
            source = right_side[level_at, 0, 0, :, col_first:col_last]
            if level_at == 0:
                residual = source
            else:
                partial_value = lift_upward(
                    masked[level_at - 1], fwd_levels[level_at - 1][panel_at][None, None]
                )
                residual = (
                    source.astype(jnp.float32) - forward_sum(partial_value, share_rows)
                ).astype(jnp.bfloat16)
            pieces.append(apply_inverse(inverse_diag[level_at, 0, 0], residual, False))
        fwd_levels.append(pieces)
    bwd_levels = [None] * levels
    for level_at in reversed(range(levels)):
        pieces = []
        panel_at = 0
        known_part = fwd_levels[level_at][panel_at]
        if level_at == levels - 1:
            residual = known_part
        else:
            partial_value = carry_downward(
                masked[level_at], bwd_levels[level_at + 1][panel_at][None, None]
            )
            residual = (
                known_part.astype(jnp.float32) - backward_sum(partial_value, share_rows)
            ).astype(jnp.bfloat16)
        pieces.append(apply_inverse(inverse_diag[level_at, 0, 0], residual, True))
        bwd_levels[level_at] = pieces
    forward_rows = []
    backward_rows = []
    for level_at in range(levels):
        forward_rows.append(jnp.concatenate(fwd_levels[level_at], axis=1))
        backward_rows.append(jnp.concatenate(bwd_levels[level_at], axis=1))
    forward_solution = jnp.stack(forward_rows).reshape(levels, 1, 1, share_rows, rhs_cols)
    solution = jnp.stack(backward_rows).reshape(levels, 1, 1, share_rows, rhs_cols)
    return (forward_solution, solution)


def solution(mesh):
    placed = (
        P(None, "row", ("depth", "col"), None, None),
        P(None, "row", ("depth", "col"), None, None, None),
        P(None, "row", None, ("depth", "col"), None),
        P(None, "row", None, ("depth", "col"), None),
    )
    return jax.shard_map(
        body,
        mesh=mesh,
        in_specs=placed,
        out_specs=(
            P(None, "row", ("depth", "col"), None, None),
            P(None, "row", ("depth", "col"), None, None),
        ),
        check_vma=False,
    )
```

profile of v0, /device:TPU:0, one launch (start us, length us, event | category | flops | bytes accessed | tf_op | source)
XLA Modules:
  0.0 735.9 jit_solution(18099699853977080136)
XLA Ops:
  7.2 1.8 convolution_convert_fusion.10
  9.8 2.6 mul.62
  12.3 7.3 mul.63
  19.6 2.6 mul.71
  22.2 7.3 mul.72
  29.6 2.6 mul.67
  32.2 7.4 mul.68
  39.5 13.6 %slice_multiply_fusion.2 = (bf16[1,1,1024,1,2048]{4,2,3,1,0:T(8,128)(2,1)}, bf16[1,1,1024,1,2048]{4,2,3,1,0:T(8,128)(2,1)}, bf16[1,1,1024,1,2048]{4,2,3,1,0:T(8,128)(2,1)}) fusion(bf16[1,1,1024,1,2048]{4,2,3,1,0:T(8,128)(2,1)} %mul.63, bf16[3,1,1024,1,2048]{4,2,3,1,0:T(8,128)(2,1)} %param.6, bf16[1,1,1024,1,2048]{4,2,3,1,0:T(8,128)(2,1)} %mul.72, ...), kind=kLoop, calls=%fused_computation.8 | loop fusion | flops 6291456 | bytes 37748736 | tf_op jit(solution)/shard_map/mul | solution.py:57
  53.1 5.1 all-gather.13.cloned.1.call-done
  58.2 6.2 fusion.9
  64.5 62.1 %all-reduce.7.cloned.1.call-done = bf16[8,128,512]{2,1,0:T(8,128)(2,1)} async-done(((bf16[8,128,512]{2,1,0:T(8,128)(2,1)}), bf16[8,128,512]{2,1,0:T(8,128)(2,1)}) %all-reduce.7.cloned.1.call-update) | async-done | bytes 1048592 | tf_op jit(solution)/shard_map/psum | solution.py:37
  126.6 1.7 convolution_convert_fusion.5
  128.5 45.3 %all-gather.15.cloned.1.call-done = bf16[2048,512]{1,0:T(8,128)(2,1)} async-done(((bf16[128,512]{1,0:T(8,128)(2,1)}), bf16[2048,512]{1,0:T(8,128)(2,1)}) %all-gather.15.cloned.1.call-update) | async-done | bytes 2097168 | tf_op jit(solution)/shard_map/all_gather | solution.py:15
  173.7 6.2 fusion.12
  180.0 62.1 %all-reduce.9.cloned.1.call-done = bf16[8,128,512]{2,1,0:T(8,128)(2,1)} async-done(((bf16[8,128,512]{2,1,0:T(8,128)(2,1)}), bf16[8,128,512]{2,1,0:T(8,128)(2,1)}) %all-reduce.9.cloned.1.call-update) | async-done | bytes 1048592 | tf_op jit(solution)/shard_map/psum | solution.py:37
  243.9 44.5 %all-gather.17.cloned.1.call-done = bf16[2048,512]{1,0:T(8,128)(2,1)} async-done(((bf16[128,512]{1,0:T(8,128)(2,1)}), bf16[2048,512]{1,0:T(8,128)(2,1)}) %all-gather.17.cloned.1.call-update) | async-done | bytes 2097168 | tf_op jit(solution)/shard_map/all_gather | solution.py:15
  288.5 6.2 fusion.15
  294.7 62.1 %all-reduce.11.cloned.1.call-done = bf16[8,128,512]{2,1,0:T(8,128)(2,1)} async-done(((bf16[8,128,512]{2,1,0:T(8,128)(2,1)}), bf16[8,128,512]{2,1,0:T(8,128)(2,1)}) %all-reduce.11.cloned.1.call-update) | async-done | bytes 1048592 | tf_op jit(solution)/shard_map/psum | solution.py:37
  359.0 15.1 %fusion.2 = (bf16[2048,1024]{0,1:T(8,128)(2,1)}, bf16[2048,1024]{0,1:T(8,128)(2,1)}, bf16[2048,1024]{0,1:T(8,128)(2,1)}) fusion(bf16[128,8,16,128]{3,2,1,0:T(8,128)(2,1)} %bitcast.180, bf16[3,1,1024,1,2048]{4,2,3,1,0:T(8,128)(2,1)} %param.6, bf16[128,8,16,128]{3,2,1,0:T(8,128)(2,1)} %bitcast.182, bf16[128,8,16,128]{3,2,1,0:T(8,128)(2,1)} %bitcast.181), kind=kLoop, calls=%fused_computation.5 | loop fusion | flops 6291456 | bytes 37748736 | tf_op jit(solution)/shard_map/dot_general | solution.py:25
  374.1 6.4 copy.26
  381.6 6.3 convolution_convert_fusion.2
  387.9 92.3 %all-reduce.13.cloned.1.call-done = bf16[16,128,512]{2,1,0:T(8,128)(2,1)} async-done(((bf16[16,128,512]{2,1,0:T(8,128)(2,1)}), bf16[16,128,512]{2,1,0:T(8,128)(2,1)}) %all-reduce.13.cloned.1.call-update) | async-done | bytes 2097168 | tf_op jit(solution)/shard_map/psum | solution.py:43
  480.2 1.8 convolution_convert_fusion.8
  482.1 6.4 copy.25
  488.5 16.4 %all-gather.21.cloned.1.call-done = bf16[1024,512]{0,1:T(8,128)(2,1)} async-done(((bf16[128,512]{0,1:T(8,128)(2,1)}), bf16[1024,512]{0,1:T(8,128)(2,1)}) %all-gather.21.cloned.1.call-update) | async-done | bytes 1048592 | tf_op jit(solution)/shard_map/all_gather | solution.py:23
  504.9 6.3 convolution_convert_fusion.1
  511.2 92.3 %all-reduce.15.cloned.1.call-done = bf16[16,128,512]{2,1,0:T(8,128)(2,1)} async-done(((bf16[16,128,512]{2,1,0:T(8,128)(2,1)}), bf16[16,128,512]{2,1,0:T(8,128)(2,1)}) %all-reduce.15.cloned.1.call-update) | async-done | bytes 2097168 | tf_op jit(solution)/shard_map/psum | solution.py:43
  603.5 1.8 convolution_convert_fusion.7
  605.3 6.4 copy.24
  611.7 16.4 %all-gather.23.cloned.1.call-done = bf16[1024,512]{0,1:T(8,128)(2,1)} async-done(((bf16[128,512]{0,1:T(8,128)(2,1)}), bf16[1024,512]{0,1:T(8,128)(2,1)}) %all-gather.23.cloned.1.call-update) | async-done | bytes 1048592 | tf_op jit(solution)/shard_map/all_gather | solution.py:23
  628.2 6.3 convolution_convert_fusion
  635.3 91.5 %all-reduce.17.cloned.1.call-done = bf16[16,128,512]{2,1,0:T(8,128)(2,1)} async-done(((bf16[16,128,512]{2,1,0:T(8,128)(2,1)}), bf16[16,128,512]{2,1,0:T(8,128)(2,1)}) %all-reduce.17.cloned.1.call-update) | async-done | bytes 2097168 | tf_op jit(solution)/shard_map/psum | solution.py:43
  (50 shorter events, 9.4 us)
Async XLA Ops:
  7.2 51.1 %all-gather.13.cloned.1.call-start = ((), (), s32[]{:S(2)}) async-start(), calls=%async_computation.6 | async-start | bytes 2228224 | tf_op jit(solution)/shard_map/all_gather | solution.py:15
  9.0 117.6 %all-reduce.7.cloned.1.call-start = ((), (), s32[]{:S(2)}) async-start(), calls=%async_computation | async-start | bytes 2097152 | tf_op jit(solution)/shard_map/psum | solution.py:37
  58.2 68.4 %copy-start.6 = (bf16[4,1,1,128,512]{4,3,2,1,0:T(8,128)(2,1)S(1)}, bf16[4,1,1,128,512]{4,3,2,1,0:T(8,128)(2,1)}, u32[]{:S(2)}) copy-start(bf16[4,1,1,128,512]{4,3,2,1,0:T(8,128)(2,1)} %param.4) | copy-start | bytes 1572868
  58.2 68.4 %copy-start.7 = (bf16[4,1,1,1,128,128]{5,4,3,2,1,0:T(8,128)(2,1)S(1)}, bf16[4,1,1,1,128,128]{5,4,3,2,1,0:T(8,128)(2,1)}, u32[]{:S(2)}) copy-start(bf16[4,1,1,1,128,128]{5,4,3,2,1,0:T(8,128)(2,1)} %param.5) | copy-start | bytes 393220
  64.5 109.2 %all-gather.15.cloned.1.call-start = ((), (), s32[]{:S(2)}) async-start(), calls=%async_computation.7 | async-start | bytes 2228224 | tf_op jit(solution)/shard_map/all_gather | solution.py:15
  128.4 113.7 %all-reduce.9.cloned.1.call-start = ((), (), s32[]{:S(2)}) async-start(), calls=%async_computation.1 | async-start | bytes 2097152 | tf_op jit(solution)/shard_map/psum | solution.py:37
  180.0 108.5 %all-gather.17.cloned.1.call-start = ((), (), s32[]{:S(2)}) async-start(), calls=%async_computation.8 | async-start | bytes 2228224 | tf_op jit(solution)/shard_map/all_gather | solution.py:15
  243.9 113.0 %all-reduce.11.cloned.1.call-start = ((), (), s32[]{:S(2)}) async-start(), calls=%async_computation.2 | async-start | bytes 2097152 | tf_op jit(solution)/shard_map/psum | solution.py:37
  294.7 86.9 %all-gather.19.cloned.1.call-start = ((), (), s32[]{:S(2)}) async-start(), calls=%async_computation.9 | async-start | bytes 1179648 | tf_op jit(solution)/shard_map/all_gather | solution.py:23
  358.8 121.4 %all-reduce.13.cloned.1.call-start = ((), (), s32[]{:S(2)}) async-start(), calls=%async_computation.3 | async-start | bytes 4194304 | tf_op jit(solution)/shard_map/psum | solution.py:43
  381.6 98.7 %copy-start.2 = (bf16[512,128]{0,1:T(8,128)(2,1)S(1)}, bf16[512,128]{0,1:T(8,128)(2,1)}, u32[]{:S(2)}) copy-start(bf16[512,128]{0,1:T(8,128)(2,1)} %convolution_convert_fusion.4) | copy-start | bytes 393220
  387.9 117.0 %all-gather.21.cloned.1.call-start = ((), (), s32[]{:S(2)}) async-start(), calls=%async_computation.10 | async-start | bytes 1179648 | tf_op jit(solution)/shard_map/all_gather | solution.py:23
  482.0 121.4 %all-reduce.15.cloned.1.call-start = ((), (), s32[]{:S(2)}) async-start(), calls=%async_computation.4 | async-start | bytes 4194304 | tf_op jit(solution)/shard_map/psum | solution.py:43
  504.9 98.6 %copy-start.1 = (bf16[512,128]{0,1:T(8,128)(2,1)S(1)}, bf16[512,128]{0,1:T(8,128)(2,1)}, u32[]{:S(2)}) copy-start(bf16[512,128]{0,1:T(8,128)(2,1)} %convolution_convert_fusion.5) | copy-start | bytes 393220
  511.2 117.0 %all-gather.23.cloned.1.call-start = ((), (), s32[]{:S(2)}) async-start(), calls=%async_computation.11 | async-start | bytes 1179648 | tf_op jit(solution)/shard_map/all_gather | solution.py:23
  605.3 121.5 %all-reduce.17.cloned.1.call-start = ((), (), s32[]{:S(2)}) async-start(), calls=%async_computation.5 | async-start | bytes 4194304 | tf_op jit(solution)/shard_map/psum | solution.py:43
  628.1 6.3 copy-start
  628.1 99.8 %copy-start.3 = (bf16[512,128]{1,0:T(8,128)(2,1)S(1)}, bf16[512,128]{1,0:T(8,128)(2,1)}, u32[]{:S(2)}) copy-start(bf16[512,128]{1,0:T(8,128)(2,1)} %convolution_convert_fusion.9) | copy-start | bytes 393220
  628.1 99.8 %copy-start.4 = (bf16[512,128]{1,0:T(8,128)(2,1)S(1)}, bf16[512,128]{1,0:T(8,128)(2,1)}, u32[]{:S(2)}) copy-start(bf16[512,128]{1,0:T(8,128)(2,1)} %convolution_convert_fusion.8) | copy-start | bytes 393220
  628.2 99.8 %copy-start.5 = (bf16[512,128]{1,0:T(8,128)(2,1)S(1)}, bf16[512,128]{1,0:T(8,128)(2,1)}, u32[]{:S(2)}) copy-start(bf16[512,128]{1,0:T(8,128)(2,1)} %convolution_convert_fusion.7) | copy-start | bytes 393220
Sparse Core Ops, SparseCore 0:
  10.7 47.4 all-gather.12
  64.6 61.9 all-reduce.6
  129.4 44.3 all-gather.14
  180.1 61.9 all-reduce.8
  244.1 44.3 all-gather.16
  294.8 61.9 all-reduce.10
  358.9 22.6 all-gather.18
  388.0 92.1 all-reduce.12
  482.2 22.6 all-gather.20
  511.3 92.1 all-reduce.14
  605.4 22.6 all-gather.22
  634.6 92.1 all-reduce.16
where the time goes:
time: 737 us; the launch traced here: 736 us
  waiting for transfers between devices  591 us (80%)
  local copies, waits for them, and re-layouts  50 us (7%)
  matrix products  49.3 us (7%)
  other arithmetic  30.3 us (4%)
  between operations  14.3 us (2%)
    psum x3, waiting for transfers between devices, backward_sum(): summed = lax.psum(blocks.astype(jnp.bfloat16), 'row').astype(jnp.float32)  276 us
    psum x3, waiting for transfers between devices, forward_sum(): lax.psum(blocks.astype(jnp.bfloat16), ('depth', 'col')).astype(jnp.float32)  186 us
    all_gather x3, waiting for transfers between devices, lift_upward(): portion = lax.all_gather(share_in, 'row', axis=0, tiled=True)  94.9 us
    all_gather x3, waiting for transfers between devices, carry_downward(): portion = lax.all_gather(share_in, ('depth', 'col'), axis=1, tiled=True)  33.9 us
    mul x6, local copies, waits for them, and re-layouts, body(): slab.reshape(gate.shape[0], block_width, gate.shape[1], block_width)  29.7 us
    dot_general x3, local copies, waits for them, and re-layouts, carry_downward(): lax.dot_general(masked, portion.reshape(span_rows, portion.shape[-1]), ((...  19.2 us
    dot_general x3, matrix products, carry_downward(): lax.dot_general(masked, portion.reshape(span_rows, portion.shape[-1]), ((...  18.8 us
    dot_general x3, matrix products, lift_upward(): jnp.dot(masked, portion.reshape(span_rows, portion.shape[-1]), preferred_...  18.6 us
  transfers between devices with their start and end apart: 12, of which 12 were waited for; matrix products, arithmetic and copies ran while one was open for 11% of the time, Pallas kernels for 0%

commit v1 on v0

--- a/solution.py
+++ b/solution.py
@@ -34,7 +34,7 @@
     blocks = partial_value.reshape(
         lax.axis_size(("depth", "col")), share_rows, partial_value.shape[-1]
     )
-    summed = lax.psum(blocks.astype(jnp.bfloat16), ("depth", "col")).astype(jnp.float32)
+    summed = lax.psum(lax.psum(blocks.astype(jnp.bfloat16), "depth"), "col").astype(jnp.float32)
     return lax.dynamic_index_in_dim(summed, lax.axis_index(("depth", "col")), 0, keepdims=False)
 
 

time: 737 us -> 778 us (1.056)
  waiting for transfers between devices: 591 us -> 632 us
    psum x3 -> x6, waiting for transfers between devices: 186 us -> 222 us  [the longest x3 149 us: forward_sum(): lax.psum(lax.psum(blocks.astype(jnp.bfloat16), 'depth'), 'col')]
  transfers between devices with their start and end apart: 12 -> 15, of which waited for: 12 -> 15; matrix products, arithmetic and copies ran while one was open for 11% -> 10% of each run, Pallas kernels for 0% -> 0%
where the time goes in v1:
time: 778 us; the launch traced here: 777 us
  waiting for transfers between devices  632 us (81%)
  local copies, waits for them, and re-layouts  50 us (6%)
  matrix products  49.3 us (6%)
  other arithmetic  30.3 us (4%)
  between operations  14 us (2%)
    psum x3, waiting for transfers between devices, backward_sum(): summed = lax.psum(blocks.astype(jnp.bfloat16), 'row').astype(jnp.float32)  276 us
    psum x3, waiting for transfers between devices, forward_sum(): lax.psum(lax.psum(blocks.astype(jnp.bfloat16), 'depth'), 'col')  149 us
    all_gather x3, waiting for transfers between devices, lift_upward(): portion = lax.all_gather(share_in, 'row', axis=0, tiled=True)  98.1 us
    psum x3, waiting for transfers between devices, forward_sum(): lax.psum(blocks.astype(jnp.bfloat16), 'depth')  73.1 us
    all_gather x3, waiting for transfers between devices, carry_downward(): portion = lax.all_gather(share_in, ('depth', 'col'), axis=1, tiled=True)  35.5 us
    mul x6, local copies, waits for them, and re-layouts, body(): slab.reshape(gate.shape[0], block_width, gate.shape[1], block_width)  29.7 us
    dot_general x3, local copies, waits for them, and re-layouts, carry_downward(): lax.dot_general(masked, portion.reshape(span_rows, portion.shape[-1]), ((...  19.2 us
    dot_general x3, matrix products, carry_downward(): lax.dot_general(masked, portion.reshape(span_rows, portion.shape[-1]), ((...  18.8 us
  transfers between devices with their start and end apart: 15, of which 15 were waited for; matrix products, arithmetic and copies ran while one was open for 10% of the time, Pallas kernels for 0%

profile of v1, /device:TPU:0, one launch (start us, length us, event | category | flops | bytes accessed | tf_op | source)
XLA Modules:
  0.0 776.6 jit_solution(6335889871753872600)
XLA Ops:
  9.8 2.6 mul.62
  12.3 7.3 mul.63
  19.6 2.6 mul.71
  22.2 7.3 mul.72
  29.6 2.6 mul.67
  32.2 7.4 mul.68
  39.5 13.6 %slice_multiply_fusion.2 = (bf16[1,1,1024,1,2048]{4,2,3,1,0:T(8,128)(2,1)}, bf16[1,1,1024,1,2048]{4,2,3,1,0:T(8,128)(2,1)}, bf16[1,1,1024,1,2048]{4,2,3,1,0:T(8,128)(2,1)}) fusion(bf16[1,1,1024,1,2048]{4,2,3,1,0:T(8,128)(2,1)} %mul.63, bf16[3,1,1024,1,2048]{4,2,3,1,0:T(8,128)(2,1)} %param.6, bf16[1,1,1024,1,2048]{4,2,3,1,0:T(8,128)(2,1)} %mul.72, ...), kind=kLoop, calls=%fused_computation.8 | loop fusion | flops 6291456 | bytes 37748736 | tf_op jit(solution)/shard_map/mul | solution.py:57
  53.1 5.1 all-gather.13.cloned.1.call-done
  58.2 6.2 fusion.9
  64.5 24.3 %all-reduce.10.cloned.1.call-done = bf16[8,128,512]{2,1,0:T(8,128)(2,1)} async-done(((bf16[8,128,512]{2,1,0:T(8,128)(2,1)}), bf16[8,128,512]{2,1,0:T(8,128)(2,1)}) %all-reduce.10.cloned.1.call-update) | async-done | bytes 1048592 | tf_op jit(solution)/shard_map/psum | solution.py:37
  89.0 49.8 %all-reduce.12.cloned.1.call-done = bf16[8,128,512]{2,1,0:T(8,128)(2,1)} async-done(((bf16[8,128,512]{2,1,0:T(8,128)(2,1)}), bf16[8,128,512]{2,1,0:T(8,128)(2,1)}) %all-reduce.12.cloned.1.call-update) | async-done | bytes 1048592 | tf_op jit(solution)/shard_map/psum | solution.py:37
  140.6 46.7 %all-gather.15.cloned.1.call-done = bf16[2048,512]{1,0:T(8,128)(2,1)} async-done(((bf16[128,512]{1,0:T(8,128)(2,1)}), bf16[2048,512]{1,0:T(8,128)(2,1)}) %all-gather.15.cloned.1.call-update) | async-done | bytes 2097168 | tf_op jit(solution)/shard_map/all_gather | solution.py:15
  187.3 6.2 fusion.12
  193.6 24.4 %all-reduce.14.cloned.1.call-done = bf16[8,128,512]{2,1,0:T(8,128)(2,1)} async-done(((bf16[8,128,512]{2,1,0:T(8,128)(2,1)}), bf16[8,128,512]{2,1,0:T(8,128)(2,1)}) %all-reduce.14.cloned.1.call-update) | async-done | bytes 1048592 | tf_op jit(solution)/shard_map/psum | solution.py:37
  218.0 49.7 %all-reduce.16.cloned.1.call-done = bf16[8,128,512]{2,1,0:T(8,128)(2,1)} async-done(((bf16[8,128,512]{2,1,0:T(8,128)(2,1)}), bf16[8,128,512]{2,1,0:T(8,128)(2,1)}) %all-reduce.16.cloned.1.call-update) | async-done | bytes 1048592 | tf_op jit(solution)/shard_map/psum | solution.py:37
  269.5 46.3 %all-gather.17.cloned.1.call-done = bf16[2048,512]{1,0:T(8,128)(2,1)} async-done(((bf16[128,512]{1,0:T(8,128)(2,1)}), bf16[2048,512]{1,0:T(8,128)(2,1)}) %all-gather.17.cloned.1.call-update) | async-done | bytes 2097168 | tf_op jit(solution)/shard_map/all_gather | solution.py:15
  315.8 6.2 fusion.15
  322.0 24.4 %all-reduce.18.cloned.1.call-done = bf16[8,128,512]{2,1,0:T(8,128)(2,1)} async-done(((bf16[8,128,512]{2,1,0:T(8,128)(2,1)}), bf16[8,128,512]{2,1,0:T(8,128)(2,1)}) %all-reduce.18.cloned.1.call-update) | async-done | bytes 1048592 | tf_op jit(solution)/shard_map/psum | solution.py:37
  346.5 49.8 %all-reduce.20.cloned.1.call-done = bf16[8,128,512]{2,1,0:T(8,128)(2,1)} async-done(((bf16[8,128,512]{2,1,0:T(8,128)(2,1)}), bf16[8,128,512]{2,1,0:T(8,128)(2,1)}) %all-reduce.20.cloned.1.call-update) | async-done | bytes 1048592 | tf_op jit(solution)/shard_map/psum | solution.py:37
  398.5 15.0 %fusion.2 = (bf16[2048,1024]{0,1:T(8,128)(2,1)}, bf16[2048,1024]{0,1:T(8,128)(2,1)}, bf16[2048,1024]{0,1:T(8,128)(2,1)}) fusion(bf16[128,8,16,128]{3,2,1,0:T(8,128)(2,1)} %bitcast.180, bf16[3,1,1024,1,2048]{4,2,3,1,0:T(8,128)(2,1)} %param.6, bf16[128,8,16,128]{3,2,1,0:T(8,128)(2,1)} %bitcast.182, bf16[128,8,16,128]{3,2,1,0:T(8,128)(2,1)} %bitcast.181), kind=kLoop, calls=%fused_computation.5 | loop fusion | flops 6291456 | bytes 37748736 | tf_op jit(solution)/shard_map/dot_general | solution.py:25
  413.5 6.4 copy.26
  419.9 2.7 all-gather.19.cloned.1.call-done
  422.6 6.3 convolution_convert_fusion.2
  429.0 92.3 %all-reduce.22.cloned.1.call-done = bf16[16,128,512]{2,1,0:T(8,128)(2,1)} async-done(((bf16[16,128,512]{2,1,0:T(8,128)(2,1)}), bf16[16,128,512]{2,1,0:T(8,128)(2,1)}) %all-reduce.22.cloned.1.call-update) | async-done | bytes 2097168 | tf_op jit(solution)/shard_map/psum | solution.py:43
  523.1 6.4 copy.25
  529.5 16.4 %all-gather.21.cloned.1.call-done = bf16[1024,512]{0,1:T(8,128)(2,1)} async-done(((bf16[128,512]{0,1:T(8,128)(2,1)}), bf16[1024,512]{0,1:T(8,128)(2,1)}) %all-gather.21.cloned.1.call-update) | async-done | bytes 1048592 | tf_op jit(solution)/shard_map/all_gather | solution.py:23
  545.9 6.3 convolution_convert_fusion.1
  552.3 92.3 %all-reduce.24.cloned.1.call-done = bf16[16,128,512]{2,1,0:T(8,128)(2,1)} async-done(((bf16[16,128,512]{2,1,0:T(8,128)(2,1)}), bf16[16,128,512]{2,1,0:T(8,128)(2,1)}) %all-reduce.24.cloned.1.call-update) | async-done | bytes 2097168 | tf_op jit(solution)/shard_map/psum | solution.py:43
  646.4 6.4 copy.24
  652.8 16.4 %all-gather.23.cloned.1.call-done = bf16[1024,512]{0,1:T(8,128)(2,1)} async-done(((bf16[128,512]{0,1:T(8,128)(2,1)}), bf16[1024,512]{0,1:T(8,128)(2,1)}) %all-gather.23.cloned.1.call-update) | async-done | bytes 1048592 | tf_op jit(solution)/shard_map/all_gather | solution.py:23
  669.2 6.3 convolution_convert_fusion
  676.4 91.5 %all-reduce.26.cloned.1.call-done = bf16[16,128,512]{2,1,0:T(8,128)(2,1)} async-done(((bf16[16,128,512]{2,1,0:T(8,128)(2,1)}), bf16[16,128,512]{2,1,0:T(8,128)(2,1)}) %all-reduce.26.cloned.1.call-update) | async-done | bytes 2097168 | tf_op jit(solution)/shard_map/psum | solution.py:43
  (59 shorter events, 15.6 us)
Async XLA Ops:
  7.2 51.1 %all-gather.13.cloned.1.call-start = ((), (), s32[]{:S(2)}) async-start(), calls=%async_computation.9 | async-start | bytes 2228224 | tf_op jit(solution)/shard_map/all_gather | solution.py:15
  9.0 79.9 %all-reduce.10.cloned.1.call-start = ((), (), s32[]{:S(2)}) async-start(), calls=%async_computation | async-start | bytes 2097152 | tf_op jit(solution)/shard_map/psum | solution.py:37
  58.2 80.5 %copy-start.6 = (bf16[4,1,1,128,512]{4,3,2,1,0:T(8,128)(2,1)S(1)}, bf16[4,1,1,128,512]{4,3,2,1,0:T(8,128)(2,1)}, u32[]{:S(2)}) copy-start(bf16[4,1,1,128,512]{4,3,2,1,0:T(8,128)(2,1)} %param.4) | copy-start | bytes 1572868
  58.2 80.5 %copy-start.7 = (bf16[4,1,1,1,128,128]{5,4,3,2,1,0:T(8,128)(2,1)S(1)}, bf16[4,1,1,1,128,128]{5,4,3,2,1,0:T(8,128)(2,1)}, u32[]{:S(2)}) copy-start(bf16[4,1,1,1,128,128]{5,4,3,2,1,0:T(8,128)(2,1)} %param.5) | copy-start | bytes 393220
  64.5 74.3 %all-reduce.12.cloned.1.call-start = ((), (), s32[]{:S(2)}) async-start(), calls=%async_computation.1 | async-start | bytes 2097152 | tf_op jit(solution)/shard_map/psum | solution.py:37
  88.9 98.4 %all-gather.15.cloned.1.call-start = ((), (), s32[]{:S(2)}) async-start(), calls=%async_computation.10 | async-start | bytes 2228224 | tf_op jit(solution)/shard_map/all_gather | solution.py:15
  140.5 77.4 %all-reduce.14.cloned.1.call-start = ((), (), s32[]{:S(2)}) async-start(), calls=%async_computation.2 | async-start | bytes 2097152 | tf_op jit(solution)/shard_map/psum | solution.py:37
  193.5 74.2 %all-reduce.16.cloned.1.call-start = ((), (), s32[]{:S(2)}) async-start(), calls=%async_computation.3 | async-start | bytes 2097152 | tf_op jit(solution)/shard_map/psum | solution.py:37
  218.0 97.8 %all-gather.17.cloned.1.call-start = ((), (), s32[]{:S(2)}) async-start(), calls=%async_computation.11 | async-start | bytes 2228224 | tf_op jit(solution)/shard_map/all_gather | solution.py:15
  269.4 77.0 %all-reduce.18.cloned.1.call-start = ((), (), s32[]{:S(2)}) async-start(), calls=%async_computation.4 | async-start | bytes 2097152 | tf_op jit(solution)/shard_map/psum | solution.py:37
  322.0 74.3 %all-reduce.20.cloned.1.call-start = ((), (), s32[]{:S(2)}) async-start(), calls=%async_computation.5 | async-start | bytes 2097152 | tf_op jit(solution)/shard_map/psum | solution.py:37
  346.4 76.2 %all-gather.19.cloned.1.call-start = ((), (), s32[]{:S(2)}) async-start(), calls=%async_computation.12 | async-start | bytes 1179648 | tf_op jit(solution)/shard_map/all_gather | solution.py:23
  398.3 123.0 %all-reduce.22.cloned.1.call-start = ((), (), s32[]{:S(2)}) async-start(), calls=%async_computation.6 | async-start | bytes 4194304 | tf_op jit(solution)/shard_map/psum | solution.py:43
  422.6 98.7 %copy-start.2 = (bf16[512,128]{0,1:T(8,128)(2,1)S(1)}, bf16[512,128]{0,1:T(8,128)(2,1)}, u32[]{:S(2)}) copy-start(bf16[512,128]{0,1:T(8,128)(2,1)} %convolution_convert_fusion.4) | copy-start | bytes 393220
  428.9 117.0 %all-gather.21.cloned.1.call-start = ((), (), s32[]{:S(2)}) async-start(), calls=%async_computation.13 | async-start | bytes 1179648 | tf_op jit(solution)/shard_map/all_gather | solution.py:23
  523.1 121.4 %all-reduce.24.cloned.1.call-start = ((), (), s32[]{:S(2)}) async-start(), calls=%async_computation.7 | async-start | bytes 4194304 | tf_op jit(solution)/shard_map/psum | solution.py:43
  545.9 98.6 %copy-start.1 = (bf16[512,128]{0,1:T(8,128)(2,1)S(1)}, bf16[512,128]{0,1:T(8,128)(2,1)}, u32[]{:S(2)}) copy-start(bf16[512,128]{0,1:T(8,128)(2,1)} %convolution_convert_fusion.5) | copy-start | bytes 393220
  552.2 117.0 %all-gather.23.cloned.1.call-start = ((), (), s32[]{:S(2)}) async-start(), calls=%async_computation.14 | async-start | bytes 1179648 | tf_op jit(solution)/shard_map/all_gather | solution.py:23
  646.3 121.5 %all-reduce.26.cloned.1.call-start = ((), (), s32[]{:S(2)}) async-start(), calls=%async_computation.8 | async-start | bytes 4194304 | tf_op jit(solution)/shard_map/psum | solution.py:43
  669.2 6.3 copy-start
  669.2 99.8 %copy-start.3 = (bf16[512,128]{1,0:T(8,128)(2,1)S(1)}, bf16[512,128]{1,0:T(8,128)(2,1)}, u32[]{:S(2)}) copy-start(bf16[512,128]{1,0:T(8,128)(2,1)} %convolution_convert_fusion.9) | copy-start | bytes 393220
  669.2 99.8 %copy-start.4 = (bf16[512,128]{1,0:T(8,128)(2,1)S(1)}, bf16[512,128]{1,0:T(8,128)(2,1)}, u32[]{:S(2)}) copy-start(bf16[512,128]{1,0:T(8,128)(2,1)} %convolution_convert_fusion.8) | copy-start | bytes 393220
  669.2 99.8 %copy-start.5 = (bf16[512,128]{1,0:T(8,128)(2,1)S(1)}, bf16[512,128]{1,0:T(8,128)(2,1)}, u32[]{:S(2)}) copy-start(bf16[512,128]{1,0:T(8,128)(2,1)} %convolution_convert_fusion.7) | copy-start | bytes 393220
Sparse Core Ops, SparseCore 0:
  10.7 47.4 all-gather.12
  64.6 24.2 all-reduce.9
  91.2 47.4 all-reduce.11
  141.3 45.9 all-gather.14
  193.6 24.2 all-reduce.13
  220.1 47.4 all-reduce.15
  269.8 45.9 all-gather.16
  322.1 24.2 all-reduce.17
  348.8 47.4 all-reduce.19
  398.4 24.1 all-gather.18
  429.0 92.1 all-reduce.21
  523.2 22.6 all-gather.20
  552.3 92.1 all-reduce.23
  646.4 22.6 all-gather.22
  675.6 92.1 all-reduce.25
